TPU v7x, 32 devices: a whole 2x2x4 slice. The times are simulated.
32 devices in a mesh: chip: 2 (over y), board: 4 (over z), cuts: 4 (over x, core).
Axes of the slice: x: 2, y: 2, z: 4, core: 2. Of those that a mesh axis runs over, the one named last changes fastest.
Arguments:
- features: bfloat16 [32, 2048, 1024], P(('chip', 'board', 'cuts')), may hold values from -6 to 6
- targets: bfloat16 [32, 2048, 256], P(('chip', 'board', 'cuts')), may hold values from -24 to 24
- lower_weight: bfloat16 [32, 1024, 512], P(('chip', 'board', 'cuts')), may hold values from -0.1875 to 0.1875
- head_weight: float32 [32, 512, 256], P(('chip', 'board', 'cuts')), may hold values from -0.25 to 0.25
- batch_rows: int32 [32, 2, 1024], P(('chip', 'board', 'cuts')), may hold values from 0 to 2047
- sample_counts: int32 [32], P(('chip', 'board', 'cuts')), may hold values from 1 to 1000
- cluster_ids: int32 [32], P(('chip', 'board', 'cuts')), may hold values from 0 to 7, as said below
Outputs:
- cluster_step: float32 [32, 512, 256], P(('chip', 'board', 'cuts'))
Inputs may be any that keep to these rules, and one draw needn't show every extreme that they name: `cluster_ids`: every one of the 8 clusters has at least one client.
All inputs are finite; a program needn't handle non-finite values.
Results may differ from a plain program's by a relative error of at most 0.0003.
Values sent between devices are 32-bit elements; how exact they have to be, the bound alone decides.
A program may use at most 64 MiB of HBM per device.

v0:
```python
import functools

import jax
import jax.numpy as jnp
from jax import lax
from jax.experimental import pallas as pl
from jax.experimental.pallas import tpu as pltpu
from jax.sharding import PartitionSpec as P

LR = 0.5
CLUSTERS = 8
LANES = 128
TILE = 256
CHUNKS = 8
LAG = 2
MESH = pl.DeviceIdType.MESH


def halves(value):
    high = value.astype(jnp.bfloat16)
    low = (value - high.astype(jnp.float32)).astype(jnp.bfloat16)
    return high, low


def dot(a, b):
    return jnp.dot(a, b, preferred_element_type=jnp.float32)


def dot_rows(a, b):
    return lax.dot_general(a, b, (((0,), (0,)), ((), ())), preferred_element_type=jnp.float32)


def local_kernel(x_hbm, lower_ref, target_ref, head_ref, rows_ref, delta_ref, x_buf, hid_hi, hid_lo, drawn, w_hi, w_lo, x_sem):
    pool = x_buf.shape[0]
    tile = min(TILE, pool)
    tiles = pool // tile
    steps, count_rows = rows_ref.shape[1], rows_ref.shape[2]
    width = head_ref.shape[2]

    def x_copy(i):
        part = pl.ds(pl.multiple_of(i * tile, tile), tile)
        return pltpu.make_async_copy(x_hbm.at[0, part], x_buf.at[part], x_sem.at[i])

    for i in range(tiles):
        x_copy(i).start()

    blocks = pool // LANES
    for step in range(steps):
        rows = rows_ref[0, step : step + 1, :]
        outer = lax.shift_right_logical(rows, 7)
        inner = lax.bitwise_and(rows, LANES - 1)
        one_outer = (lax.broadcasted_iota(jnp.int32, (blocks, count_rows), 0) == outer).astype(jnp.float32).astype(jnp.bfloat16)
        one_inner = (lax.broadcasted_iota(jnp.int32, (LANES, count_rows), 0) == inner).astype(jnp.float32).astype(jnp.bfloat16)
        table = lax.dot_general(one_inner, one_outer, (((1,), (1,)), ((), ())), preferred_element_type=jnp.float32)
        for j in range(blocks):
            drawn[step, j * LANES : (j + 1) * LANES, :] = jnp.broadcast_to(table[:, j : j + 1], (LANES, LANES))

    high, low = halves(head_ref[0])
    w_hi[...] = high
    w_lo[...] = low
    delta_ref[...] = jnp.zeros_like(delta_ref)
    scale = -LR / count_rows

    for step in range(steps):

        @pl.loop(0, tiles)
        def _(i):
            part = pl.ds(pl.multiple_of(i * tile, tile), tile)
            if step == 0:
                x_copy(i).wait()
                hidden = jnp.tanh(dot(x_buf[part, :], lower_ref[0]))
                h_hi, h_lo = halves(hidden)
                hid_hi[part, :] = h_hi
                hid_lo[part, :] = h_lo
            else:
                h_hi = hid_hi[part, :]
                h_lo = hid_lo[part, :]
            err = dot(h_hi, w_hi[...]) + dot(h_hi, w_lo[...]) + dot(h_lo, w_hi[...])
            err = err - target_ref[0, part, :].astype(jnp.float32)
            times = drawn[step, part, :]
            err = err * jnp.concatenate([times] * (width // LANES), axis=1) * scale
            e_hi, e_lo = halves(err)
            delta_ref[...] += dot_rows(h_hi, e_hi) + dot_rows(h_hi, e_lo) + dot_rows(h_lo, e_hi)

        if step + 1 < steps:
            high, low = halves(head_ref[0] + delta_ref[...])
            w_hi[...] = high
            w_lo[...] = low


def local_delta(features, targets, lower_weight, head_weight, batch_rows):
    pool, features_in = features.shape[1:]
    hid, out = head_weight.shape[1:]
    vmem = pl.BlockSpec(memory_space=pltpu.VMEM)
    tiles = pool // min(TILE, pool)
    return pl.pallas_call(
        local_kernel,
        name="local_steps",
        out_shape=jax.ShapeDtypeStruct((hid, out), jnp.float32),
        in_specs=[pl.BlockSpec(memory_space=pl.ANY), vmem, vmem, vmem, vmem],
        out_specs=vmem,
        scratch_shapes=[
            pltpu.VMEM((pool, features_in), jnp.bfloat16),
            pltpu.VMEM((pool, hid), jnp.bfloat16),
            pltpu.VMEM((pool, hid), jnp.bfloat16),
            pltpu.VMEM((batch_rows.shape[1], pool, LANES), jnp.float32),
            pltpu.VMEM((hid, out), jnp.bfloat16),
            pltpu.VMEM((hid, out), jnp.bfloat16),
            pltpu.SemaphoreType.DMA((tiles,)),
        ],
        compiler_params=pltpu.CompilerParams(vmem_limit_bytes=40 * 2**20),
    )(features, lower_weight, targets, head_weight, batch_rows)


def mean_kernel(
    sizes, chunks, id_ref, count_ref, delta_ref, out_ref,
    facts, chosen, inbox, own, from_left, from_right, to_right, to_left, outbox, result,
    fact_send, fact_recv, share_send, share_recv, right_send, right_recv, left_send, left_recv, back_send, back_recv,
):
    chip_count, board_count, cuts_count = sizes
    plane = chip_count * cuts_count
    number = plane * board_count
    chip, board, cuts = lax.axis_index("chip"), lax.axis_index("board"), lax.axis_index("cuts")
    seat = chip * cuts_count + cuts
    me = board * plane + seat
    hid, width = delta_ref.shape
    block = hid // chunks
    share = block // plane

    def at(board_index, seat_index):
        return (seat_index // cuts_count, board_index, lax.rem(seat_index, cuts_count))

    def rows_of(k, seat_index):
        return pl.ds(pl.multiple_of(k * block + seat_index * share, 8), share)

    barrier = pltpu.get_barrier_semaphore()

    def greet(offset, carry):
        other = lax.rem(me + offset, number)
        pl.semaphore_signal(barrier, inc=1, device_id=at(other // plane, lax.rem(other, plane)), device_id_type=MESH)
        return carry

    lax.fori_loop(1, number, greet, 0)
    kind = lax.broadcasted_iota(jnp.int32, (CLUSTERS, LANES), 0)
    facts[me] = jnp.where(kind == id_ref[0], count_ref[0].astype(jnp.float32), 0.0)
    pl.semaphore_wait(barrier, number - 1)

    def tell(offset, carry):
        other = lax.rem(me + offset, number)
        pltpu.make_async_remote_copy(
            src_ref=facts.at[me], dst_ref=facts.at[me], send_sem=fact_send, recv_sem=fact_recv,
            device_id=at(other // plane, lax.rem(other, plane)), device_id_type=MESH,
        ).start()
        return carry

    lax.fori_loop(1, number, tell, 0)

    for k in range(chunks):

        def give(offset, carry, k=k):
            other = lax.rem(seat + offset, plane)
            pltpu.make_async_remote_copy(
                src_ref=delta_ref.at[rows_of(k, other)], dst_ref=inbox.at[k, seat],
                send_sem=share_send, recv_sem=share_recv.at[k],
                device_id=at(board, other), device_id_type=MESH,
            ).start()
            return carry

        lax.fori_loop(1, plane, give, 0)
        inbox[k, seat] = delta_ref[rows_of(k, seat), :]

    def arrived(ref, sem):
        pltpu.make_async_copy(ref, ref, sem).wait()

    arrived(facts.at[pl.ds(0, number - 1)], fact_recv)
    counts = jnp.sum(facts[...], axis=0)
    inverse = 1.0 / (LR * jnp.maximum(counts, 1.0))
    for t in range(plane):
        chosen[t] = jnp.where(facts[board * plane + t] > 0, inverse, 0.0)

    def wide(row):
        return jnp.concatenate([row] * (width // LANES), axis=1)

    def right_copy(k):
        return pltpu.make_async_remote_copy(
            src_ref=to_right.at[k], dst_ref=from_left.at[k], send_sem=right_send.at[k], recv_sem=right_recv.at[k],
            device_id=at(board + 1, seat), device_id_type=MESH,
        )

    def left_copy(k):
        return pltpu.make_async_remote_copy(
            src_ref=to_left.at[k], dst_ref=from_right.at[k], send_sem=left_send.at[k], recv_sem=left_recv.at[k],
            device_id=at(board - 1, seat), device_id_type=MESH,
        )

    last = board_count - 1

    def add_up(k):
        arrived(inbox.at[k, pl.ds(0, plane - 1)], share_recv.at[k])
        sums = [jnp.zeros((share, width), jnp.float32)] * CLUSTERS
        for t in range(plane):
            value = inbox[k, t]
            for c in range(CLUSTERS):
                sums[c] = sums[c] + wide(facts[board * plane + t, c : c + 1, :]) * value
        for c in range(CLUSTERS):
            own[k, c] = sums[c]

    def pass_right(k):
        @pl.when(board == 0)
        def _():
            from_left[k] = jnp.zeros_like(from_left[k])

        @pl.when(board > 0)
        def _():
            arrived(from_left.at[k], right_recv.at[k])

        @pl.when(board < last)
        def _():
            to_right[k] = own[k] + from_left[k]
            right_copy(k).start()

    def pass_left(k):
        @pl.when(board == last)
        def _():
            from_right[k] = jnp.zeros_like(from_right[k])

        @pl.when(board < last)
        def _():
            arrived(from_right.at[k], left_recv.at[k])

        @pl.when(board > 0)
        def _():
            to_left[k] = own[k] + from_right[k]
            left_copy(k).start()

    def give_back(k):
        total = [own[k, c] + from_left[k, c] + from_right[k, c] for c in range(CLUSTERS)]
        for t in range(plane):
            value = wide(chosen[t, 0:1, :]) * total[0]
            for c in range(1, CLUSTERS):
                value = value + wide(chosen[t, c : c + 1, :]) * total[c]
            outbox[k, t] = value
        result[rows_of(k, seat), :] = outbox[k, seat]

        def give(offset, carry):
            other = lax.rem(seat + offset, plane)
            pltpu.make_async_remote_copy(
                src_ref=outbox.at[k, other], dst_ref=result.at[rows_of(k, seat)],
                send_sem=back_send, recv_sem=back_recv,
                device_id=at(board, other), device_id_type=MESH,
            ).start()
            return carry

        lax.fori_loop(1, plane, give, 0)

    right_lag = LAG * board
    left_lag = LAG * (last - board)
    back_lag = jnp.maximum(right_lag, left_lag)

    def tick(step, carry):
        for lag, act in ((0, add_up), (right_lag, pass_right), (left_lag, pass_left), (back_lag, give_back)):
            k = step - lag

            @pl.when((k >= 0) & (k < chunks))
            def _():
                act(k)

        return carry

    lax.fori_loop(0, chunks + LAG * last, tick, 0)

    moved = pl.ds(0, chunks * (plane - 1) * share)
    arrived(result.at[moved], back_recv)
    out_ref[0] = result[...]
    arrived(result.at[moved], back_send)
    arrived(result.at[moved], share_send)
    arrived(facts.at[pl.ds(0, number - 1)], fact_send)

    @pl.when(board < last)
    def _():
        for k in range(chunks):
            arrived(to_right.at[k], right_send.at[k])

    @pl.when(board > 0)
    def _():
        for k in range(chunks):
            arrived(to_left.at[k], left_send.at[k])


def cluster_mean(sizes, delta, sample_counts, cluster_ids):
    hid, width = delta.shape
    plane = sizes[0] * sizes[2]
    number = plane * sizes[1]
    chunks = max(1, min(CHUNKS, hid // (plane * 8)))
    share = hid // (chunks * plane)
    vmem = pl.BlockSpec(memory_space=pltpu.VMEM)
    smem = pl.BlockSpec(memory_space=pltpu.SMEM)
    sums = pltpu.VMEM((chunks, CLUSTERS, share, width), jnp.float32)
    shares = pltpu.VMEM((chunks, plane, share, width), jnp.float32)
    one, many = pltpu.SemaphoreType.DMA, pltpu.SemaphoreType.DMA((chunks,))
    return pl.pallas_call(
        functools.partial(mean_kernel, sizes, chunks),
        name="cluster_mean",
        out_shape=jax.ShapeDtypeStruct((1, hid, width), jnp.float32),
        in_specs=[smem, smem, vmem],
        out_specs=vmem,
        scratch_shapes=[
            pltpu.VMEM((number, CLUSTERS, LANES), jnp.float32),
            pltpu.VMEM((plane, CLUSTERS, LANES), jnp.float32),
            shares, sums, sums, sums, sums, sums, shares,
            pltpu.VMEM((hid, width), jnp.float32),
            one, one, one, many, many, many, many, many, one, one,
        ],
        compiler_params=pltpu.CompilerParams(collective_id=0, has_side_effects=True, vmem_limit_bytes=40 * 2**20),
    )(cluster_ids, sample_counts, delta)


def solution(mesh):
    sizes = (mesh.shape["chip"], mesh.shape["board"], mesh.shape["cuts"])

    def on_device(features, targets, lower_weight, head_weight, batch_rows, sample_counts, cluster_ids):
        delta = local_delta(features, targets, lower_weight, head_weight, batch_rows)
        return cluster_mean(sizes, delta, sample_counts, cluster_ids)

    rows, flat = P(("chip", "board", "cuts"), None, None), P(("chip", "board", "cuts"))
    return jax.shard_map(
        on_device,
        mesh=mesh,
        in_specs=(rows, rows, rows, rows, rows, flat, flat),
        out_specs=rows,
        check_vma=False,
    )
```

profile of v0, /device:TPU:0, one launch (start us, length us, event | category | flops | bytes accessed | tf_op | source)
XLA Modules:
  0.0 68.3 jit_solution(7844255217363818168)
XLA Ops:
  1.3 0.0 copy-start
  1.3 2.2 %copy-done = bf16[1,2048,1024]{2,1,0:T(8,128)(2,1)S(1)} copy-done((bf16[1,2048,1024]{2,1,0:T(8,128)(2,1)S(1)}, bf16[1,2048,1024]{2,1,0:T(8,128)(2,1)}, u32[]{:S(2)}) %copy-start) | copy-done | bytes 4194328
  3.5 0.0 copy-start.1
  3.5 1.2 %copy-done.1 = bf16[1,1024,512]{2,1,0:T(8,128)(2,1)S(1)} copy-done((bf16[1,1024,512]{2,1,0:T(8,128)(2,1)S(1)}, bf16[1,1024,512]{2,1,0:T(8,128)(2,1)}, u32[]{:S(2)}) %copy-start.1) | copy-done | bytes 1048600
  4.7 0.0 copy-start.2
  4.7 1.2 %copy-done.2 = bf16[1,2048,256]{2,1,0:T(8,128)(2,1)S(1)} copy-done((bf16[1,2048,256]{2,1,0:T(8,128)(2,1)S(1)}, bf16[1,2048,256]{2,1,0:T(8,128)(2,1)}, u32[]{:S(2)}) %copy-start.2) | copy-done | bytes 1048600
  5.9 0.0 copy-start.3
  5.9 1.0 %copy-done.3 = f32[1,512,256]{2,1,0:T(8,128)S(1)} copy-done((f32[1,512,256]{2,1,0:T(8,128)S(1)}, f32[1,512,256]{2,1,0:T(8,128)}, u32[]{:S(2)}) %copy-start.3) | copy-done | bytes 524312
  7.0 0.0 copy-start.4
  7.0 0.7 %copy-done.4 = s32[1,2,1024]{2,1,0:T(2,128)S(1)} copy-done((s32[1,2,1024]{2,1,0:T(2,128)S(1)}, s32[1,2,1024]{2,1,0:T(2,128)}, u32[]{:S(2)}) %copy-start.4) | copy-done | bytes 8216
  7.7 21.6 %local_steps.1.delta_ref = f32[512,256]{1,0:T(8,128)S(1)} custom-call(bf16[1,2048,1024]{2,1,0:T(8,128)(2,1)S(1)} %copy-done, bf16[1,1024,512]{2,1,0:T(8,128)(2,1)S(1)} %copy-done.1, bf16[1,2048,256]{2,1,0:T(8,128)(2,1)S(1)} %copy-done.2, f32[1,512,256]{2,1,0:T(8,128)S(1)} %copy-done.3, s32[1,2,1024]{2,1,0:T(2,128)S(1)} %copy-done.4), custom_call_target="tpu_custom_call" | custom-call | tf_op jit(solution)/shard_map/local_steps/pallas_call | solution.py:96
  29.3 38.2 %cluster_mean.1 = f32[1,512,256]{2,1,0:T(8,128)S(1)} custom-call(s32[1]{0:T(128)S(6)} %copy.10.id_ref, s32[1]{0:T(128)S(6)} %copy.9.count_ref, f32[512,256]{1,0:T(8,128)S(1)} %local_steps.1.delta_ref), custom_call_target="tpu_custom_call" | custom-call | tf_op jit(solution)/shard_map/cluster_mean/pallas_call | solution.py:301
  67.6 0.8 %copy.11 = f32[1,512,256]{2,1,0:T(8,128)} copy(f32[1,512,256]{2,1,0:T(8,128)S(1)} %cluster_mean.1) | data formatting | bytes 1048576
Async XLA Ops:
  1.3 2.2 %copy-start = (bf16[1,2048,1024]{2,1,0:T(8,128)(2,1)S(1)}, bf16[1,2048,1024]{2,1,0:T(8,128)(2,1)}, u32[]{:S(2)}) copy-start(bf16[1,2048,1024]{2,1,0:T(8,128)(2,1)} %x_hbm.1) | copy-start | bytes 12582916
  3.5 1.2 %copy-start.1 = (bf16[1,1024,512]{2,1,0:T(8,128)(2,1)S(1)}, bf16[1,1024,512]{2,1,0:T(8,128)(2,1)}, u32[]{:S(2)}) copy-start(bf16[1,1024,512]{2,1,0:T(8,128)(2,1)} %lower_ref.1) | copy-start | bytes 3145732
  4.7 1.2 %copy-start.2 = (bf16[1,2048,256]{2,1,0:T(8,128)(2,1)S(1)}, bf16[1,2048,256]{2,1,0:T(8,128)(2,1)}, u32[]{:S(2)}) copy-start(bf16[1,2048,256]{2,1,0:T(8,128)(2,1)} %target_ref.1) | copy-start | bytes 3145732
  5.9 1.0 %copy-start.3 = (f32[1,512,256]{2,1,0:T(8,128)S(1)}, f32[1,512,256]{2,1,0:T(8,128)}, u32[]{:S(2)}) copy-start(f32[1,512,256]{2,1,0:T(8,128)} %head_ref.1) | copy-start | bytes 1572868
  7.0 0.7 %copy-start.4 = (s32[1,2,1024]{2,1,0:T(2,128)S(1)}, s32[1,2,1024]{2,1,0:T(2,128)}, u32[]{:S(2)}) copy-start(s32[1,2,1024]{2,1,0:T(2,128)} %rows_ref.1) | copy-start | bytes 24580
where the time goes:
time: 68.7 us; the launch traced here: 68.3 us
  Pallas kernels  59.9 us (87%)
  local copies, waits for them, and re-layouts  7.16 us (10%)
  between operations  1.33 us (2%)
    pallas_call x1, Pallas kernels, cluster_mean(): pl.pallas_call(functools.partial(mean_kernel, sizes, chunks), name='clust...  38.2 us
    pallas_call x1, Pallas kernels, local_delta(): pl.pallas_call(local_kernel, name='local_steps', out_shape=jax.ShapeDtype...  21.6 us
    unnamed x11, local copies, waits for them, and re-layouts  7.16 us

commit v1 on v0

v1 whole, which is shorter than its diff:
```python
import functools

import jax
import jax.numpy as jnp
from jax import lax
from jax.experimental import pallas as pl
from jax.experimental.pallas import tpu as pltpu
from jax.sharding import PartitionSpec as P

LR = 0.5
CLUSTERS = 8
LANES = 128
TILE = 512
GRAD_ROWS = 256
SHARE = 8
LAG = 2
MESH = pl.DeviceIdType.MESH


def halves(value):
    high = value.astype(jnp.bfloat16)
    low = (value - high.astype(jnp.float32)).astype(jnp.bfloat16)
    return high, low


def dot(a, b):
    return jnp.dot(a, b, preferred_element_type=jnp.float32)


def round_kernel(
    sizes, x_hbm, lower_hbm, target_hbm, head_hbm, rows_hbm, count_ref, id_ref, out_ref,
    x_buf, lower, target, head, rows_ref, hid_hi, hid_lo, hid_t_hi, hid_t_lo, drawn, w_hi, w_lo, err_hi, err_lo, delta,
    facts, chosen, inbox, own, other, outbox, result,
    x_sem, in_sem, fact_send, fact_recv, share_send, share_recv, pair_send, pair_recv, back_send, back_recv,
):
    pool = x_buf.shape[0]
    tile = x_buf.shape[0] // x_sem.shape[0]
    tiles = pool // tile
    steps, count_rows = rows_ref.shape
    hid, width = head.shape
    chip_count, board_count, cuts_count = sizes
    plane = chip_count * cuts_count
    number = plane * board_count
    half = board_count // 2
    members = half * plane
    chunks = inbox.shape[0]
    block = hid // chunks
    share = block // plane

    chip, board, cuts = lax.axis_index("chip"), lax.axis_index("board"), lax.axis_index("cuts")
    seat = chip * cuts_count + cuts
    me = board * plane + seat
    side = (board >= half).astype(jnp.int32)
    hub = half - 1 + side
    is_hub = board == hub
    member = (board - side * half) * plane + seat

    def at(board_index, seat_index):
        return (lax.div(seat_index, cuts_count), board_index, lax.rem(seat_index, cuts_count))

    def x_copy(i):
        part = pl.ds(i * tile, tile)
        return pltpu.make_async_copy(x_hbm.at[0, part], x_buf.at[part], x_sem.at[i])

    rows_copy = pltpu.make_async_copy(rows_hbm.at[0], rows_ref, in_sem.at[0])
    lower_copy = pltpu.make_async_copy(lower_hbm.at[0], lower, in_sem.at[1])
    head_copy = pltpu.make_async_copy(head_hbm.at[0], head, in_sem.at[2])
    target_copy = pltpu.make_async_copy(target_hbm.at[0], target, in_sem.at[3])
    rows_copy.start()
    lower_copy.start()
    x_copy(0).start()
    head_copy.start()
    target_copy.start()
    for i in range(1, tiles):
        x_copy(i).start()

    barrier = pltpu.get_barrier_semaphore()

    def greet(offset, carry):
        peer = lax.rem(me + offset, number)
        pl.semaphore_signal(barrier, inc=1, device_id=at(lax.div(peer, plane), lax.rem(peer, plane)), device_id_type=MESH)
        return carry

    lax.fori_loop(1, number, greet, 0)
    kind = lax.broadcasted_iota(jnp.int32, (CLUSTERS, LANES), 0)
    facts[me] = jnp.where(kind == id_ref[0], count_ref[0].astype(jnp.float32), 0.0)

    rows_copy.wait()
    blocks = pool // LANES
    for step in range(steps):
        rows = rows_ref[step : step + 1, :]
        outer = lax.shift_right_logical(rows, 7)
        inner = lax.bitwise_and(rows, LANES - 1)
        one_outer = (lax.broadcasted_iota(jnp.int32, (blocks, count_rows), 0) == outer).astype(jnp.float32).astype(jnp.bfloat16)
        one_inner = (lax.broadcasted_iota(jnp.int32, (LANES, count_rows), 0) == inner).astype(jnp.float32).astype(jnp.bfloat16)
        table = lax.dot_general(one_inner, one_outer, (((1,), (1,)), ((), ())), preferred_element_type=jnp.float32)
        for j in range(blocks):
            drawn[step, j * LANES : (j + 1) * LANES, :] = jnp.broadcast_to(table[:, j : j + 1], (LANES, LANES))

    head_copy.wait()
    high, low = halves(head[...])
    w_hi[...] = high
    w_lo[...] = low
    lower_copy.wait()
    target_copy.wait()
    scale = -LR / count_rows

    def error(step, part, h_hi, h_lo):
        err = dot(h_hi, w_hi[...]) + dot(h_hi, w_lo[...]) + dot(h_lo, w_hi[...])
        err = err - target[part, :].astype(jnp.float32)
        err = err * jnp.concatenate([drawn[step, part, :]] * (width // LANES), axis=1) * scale
        e_hi, e_lo = halves(err)
        err_hi[part, :] = e_hi
        err_lo[part, :] = e_lo

    def gradient(part):
        return dot(hid_t_hi[part, :], err_hi[...]) + dot(hid_t_hi[part, :], err_lo[...]) + dot(hid_t_lo[part, :], err_hi[...])

    for i in range(tiles):
        part = pl.ds(i * tile, tile)
        x_copy(i).wait()
        h_hi, h_lo = halves(jnp.tanh(dot(x_buf[part, :], lower[...])))
        hid_hi[part, :] = h_hi
        hid_lo[part, :] = h_lo
        hid_t_hi[:, part] = h_hi.T
        hid_t_lo[:, part] = h_lo.T
        error(0, part, h_hi, h_lo)

    pl.semaphore_wait(barrier, number - 1)

    def tell(offset, carry):
        peer = lax.rem(seat + offset, plane)
        for where in (half - 1, half):
            @pl.when((offset > 0) | (board != where))
            def _():
                pltpu.make_async_remote_copy(
                    src_ref=facts.at[me], dst_ref=facts.at[me], send_sem=fact_send, recv_sem=fact_recv,
                    device_id=at(where, peer), device_id_type=MESH,
                ).start()
        return carry

    lax.fori_loop(0, plane, tell, 0)

    def rows_of(k, seat_index):
        return pl.ds(pl.multiple_of(k * block + seat_index * share, 8), share)

    def give_share(k, offset):
        peer = lax.rem(seat + offset, plane)
        pltpu.make_async_remote_copy(
            src_ref=delta.at[rows_of(k, peer)], dst_ref=inbox.at[k, member],
            send_sem=share_send, recv_sem=share_recv.at[k],
            device_id=at(hub, peer), device_id_type=MESH,
        ).start()

    grad_rows = min(GRAD_ROWS, hid)
    for step in range(steps):
        if step > 0:
            for i in range(tiles):
                part = pl.ds(i * tile, tile)
                error(step, part, hid_hi[part, :], hid_lo[part, :])
        for i in range(hid // grad_rows):
            part = pl.ds(i * grad_rows, grad_rows)
            value = gradient(part)
            if step > 0:
                value = value + delta[part, :]
            delta[part, :] = value
            if step + 1 < steps:
                high, low = halves(head[part, :] + value)
                w_hi[part, :] = high
                w_lo[part, :] = low
            else:
                for k in range(i * grad_rows // block, (i + 1) * grad_rows // block):
                    @pl.when(is_hub)
                    def _(k=k):
                        inbox[k, member] = delta[rows_of(k, seat), :]

                    @pl.when(jnp.logical_not(is_hub))
                    def _(k=k):
                        give_share(k, 0)

                    for offset in range(1, plane):
                        give_share(k, offset)

    def arrived(ref, sem):
        pltpu.make_async_copy(ref, ref, sem).wait()

    def wide(row):
        return jnp.concatenate([row] * (width // LANES), axis=1)

    def pair_copy(k):
        return pltpu.make_async_remote_copy(
            src_ref=own.at[k], dst_ref=other.at[k], send_sem=pair_send.at[k], recv_sem=pair_recv.at[k],
            device_id=at(board_count - 1 - hub, seat), device_id_type=MESH,
        )

    @pl.when(is_hub)
    def _():
        arrived(facts.at[pl.ds(0, number - 1)], fact_recv)
        counts = jnp.sum(facts[...], axis=0)
        inverse = 1.0 / (LR * jnp.maximum(counts, 1.0))
        first = side * members
        for t in range(members):
            chosen[t] = jnp.where(facts[first + t] > 0, inverse, 0.0)

        def add_up(k):
            arrived(inbox.at[k, pl.ds(0, members - 1)], share_recv.at[k])
            sums = [jnp.zeros((share, width), jnp.float32)] * CLUSTERS
            for t in range(members):
                value = inbox[k, t]
                for c in range(CLUSTERS):
                    sums[c] = sums[c] + wide(facts[first + t, c : c + 1, :]) * value
            for c in range(CLUSTERS):
                own[k, c] = sums[c]
            pair_copy(k).start()

        def give_back(k):
            arrived(other.at[k], pair_recv.at[k])
            total = [own[k, c] + other[k, c] for c in range(CLUSTERS)]
            for t in range(members):
                value = wide(chosen[t, 0:1, :]) * total[0]
                for c in range(1, CLUSTERS):
                    value = value + wide(chosen[t, c : c + 1, :]) * total[c]
                outbox[k, t] = value
            result[rows_of(k, seat), :] = outbox[k, member]

            def give(offset, carry):
                target_member = lax.rem(member + offset, members)
                pltpu.make_async_remote_copy(
                    src_ref=outbox.at[k, target_member], dst_ref=result.at[rows_of(k, seat)],
                    send_sem=back_send, recv_sem=back_recv,
                    device_id=at(side * half + lax.div(target_member, plane), lax.rem(target_member, plane)), device_id_type=MESH,
                ).start()
                return carry

            lax.fori_loop(1, members, give, 0)

        def tick(step, carry):
            @pl.when(step < chunks)
            def _():
                add_up(step)

            @pl.when(step >= LAG)
            def _():
                give_back(step - LAG)

            return carry

        lax.fori_loop(0, chunks + LAG, tick, 0)
        arrived(result.at[pl.ds(0, chunks * (plane - 1) * share)], back_recv)

    @pl.when(jnp.logical_not(is_hub))
    def _():
        arrived(result, back_recv)

    out_ref[0] = result[...]

    @pl.when(is_hub)
    def _():
        arrived(delta.at[pl.ds(0, chunks * (plane - 1) * share)], share_send)
        arrived(facts.at[pl.ds(0, 2 * plane - 1)], fact_send)
        for k in range(chunks):
            arrived(own.at[k], pair_send.at[k])
        arrived(outbox.at[:, pl.ds(0, members - 1)], back_send)

    @pl.when(jnp.logical_not(is_hub))
    def _():
        arrived(delta, share_send)
        arrived(facts.at[pl.ds(0, 2 * plane)], fact_send)


def federated_round(sizes, features, targets, lower_weight, head_weight, batch_rows, sample_counts, cluster_ids):
    pool, features_in = features.shape[1:]
    hid, width = head_weight.shape[1:]
    steps, count_rows = batch_rows.shape[1:]
    plane = sizes[0] * sizes[2]
    number = plane * sizes[1]
    members = number // 2
    share = SHARE
    chunks = hid // (plane * share)
    tiles = pool // min(TILE, pool)
    vmem = pl.BlockSpec(memory_space=pltpu.VMEM)
    smem = pl.BlockSpec(memory_space=pltpu.SMEM)
    hbm = pl.BlockSpec(memory_space=pltpu.HBM)
    half_type, full_type = jnp.bfloat16, jnp.float32
    one, many = pltpu.SemaphoreType.DMA, pltpu.SemaphoreType.DMA((chunks,))
    return pl.pallas_call(
        functools.partial(round_kernel, sizes),
        name="federated_round",
        out_shape=jax.ShapeDtypeStruct((1, hid, width), full_type),
        in_specs=[hbm] * 5 + [smem] * 2,
        out_specs=vmem,
        scratch_shapes=[
            pltpu.VMEM((pool, features_in), half_type),
            pltpu.VMEM((features_in, hid), half_type),
            pltpu.VMEM((pool, width), half_type),
            pltpu.VMEM((hid, width), full_type),
            pltpu.VMEM((steps, count_rows), jnp.int32),
            pltpu.VMEM((pool, hid), half_type),
            pltpu.VMEM((pool, hid), half_type),
            pltpu.VMEM((hid, pool), half_type),
            pltpu.VMEM((hid, pool), half_type),
            pltpu.VMEM((steps, pool, LANES), full_type),
            pltpu.VMEM((hid, width), half_type),
            pltpu.VMEM((hid, width), half_type),
            pltpu.VMEM((pool, width), half_type),
            pltpu.VMEM((pool, width), half_type),
            pltpu.VMEM((hid, width), full_type),
            pltpu.VMEM((number, CLUSTERS, LANES), full_type),
            pltpu.VMEM((members, CLUSTERS, LANES), full_type),
            pltpu.VMEM((chunks, members, share, width), full_type),
            pltpu.VMEM((chunks, CLUSTERS, share, width), full_type),
            pltpu.VMEM((chunks, CLUSTERS, share, width), full_type),
            pltpu.VMEM((chunks, members, share, width), full_type),
            pltpu.VMEM((hid, width), full_type),
            pltpu.SemaphoreType.DMA((tiles,)),
            pltpu.SemaphoreType.DMA((4,)),
            one, one, one, many, many, many, one, one,
        ],
        compiler_params=pltpu.CompilerParams(collective_id=0, has_side_effects=True, vmem_limit_bytes=56 * 2**20),
    )(features, lower_weight, targets, head_weight, batch_rows, sample_counts, cluster_ids)


def solution(mesh):
    sizes = (mesh.shape["chip"], mesh.shape["board"], mesh.shape["cuts"])
    rows, flat = P(("chip", "board", "cuts"), None, None), P(("chip", "board", "cuts"))
    return jax.shard_map(
        functools.partial(federated_round, sizes),
        mesh=mesh,
        in_specs=(rows, rows, rows, rows, rows, flat, flat),
        out_specs=rows,
        check_vma=False,
    )
```

time: 68.7 us -> 45 us (0.66)
  Pallas kernels: 59.9 us -> 41.6 us
  local copies, waits for them, and re-layouts: 7.16 us -> 1.87 us
    pallas_call x2 -> x1, Pallas kernels: 59.9 us -> 41.6 us  [federated_round(): pl.pallas_call(functools.partial(round_kernel, sizes), name='federated_ro...]
    unnamed x11 -> x1, local copies, waits for them, and re-layouts: 7.16 us -> 1.87 us
where the time goes in v1:
time: 45 us; the launch traced here: 44.7 us
  Pallas kernels  41.6 us (92%)
  local copies, waits for them, and re-layouts  1.87 us (4%)
  between operations  1.3 us (3%)
    pallas_call x1, Pallas kernels, federated_round(): pl.pallas_call(functools.partial(round_kernel, sizes), name='federated_ro...  41.6 us
    unnamed x1, local copies, waits for them, and re-layouts  1.87 us

profile of v1, /device:TPU:0, one launch (start us, length us, event | category | flops | bytes accessed | tf_op | source)
XLA Modules:
  0.0 44.7 jit_solution(13600708578692134825)
XLA Ops:
  1.3 41.6 %federated_round.1 = f32[1,512,256]{2,1,0:T(8,128)} custom-call(bf16[1,2048,1024]{2,1,0:T(8,128)(2,1)} %x_hbm.1, bf16[1,1024,512]{2,1,0:T(8,128)(2,1)} %lower_hbm.1, bf16[1,2048,256]{2,1,0:T(8,128)(2,1)} %target_hbm.1, f32[1,512,256]{2,1,0:T(8,128)} %head_hbm.1, s32[1,2,1024]{2,1,0:T(2,128)} %rows_hbm.1, s32[1]{0:T(128)S(6)} %copy.9.count_ref, s32[1]{0:T(128)S(6)} %copy.10.id_ref), custom_call_target="tpu_custom_call" | custom-call | tf_op jit(solution)/shard_map/federated_round/pallas_call | solution.py:286
  42.9 1.9 %copy.11 = f32[1,512,256]{2,1,0:T(8,128)} copy(f32[1,512,256]{2,1,0:T(8,128)} %federated_round.1) | data formatting | bytes 1048576

commit v2 on v1

--- a/solution.py
+++ b/solution.py
@@ -13,7 +13,10 @@
 TILE = 512
 GRAD_ROWS = 256
 SHARE = 8
-LAG = 2
+COLUMNS = 128
+LAG = 4
+LIMIT = 53
+WAIT = 1
 MESH = pl.DeviceIdType.MESH
 
 
@@ -43,9 +46,9 @@
     number = plane * board_count
     half = board_count // 2
     members = half * plane
-    chunks = inbox.shape[0]
-    block = hid // chunks
-    share = block // plane
+    chunks, _, share, columns = inbox.shape
+    groups = width // columns
+    block = plane * share
 
     chip, board, cuts = lax.axis_index("chip"), lax.axis_index("board"), lax.axis_index("cuts")
     seat = chip * cuts_count + cuts
@@ -53,10 +56,39 @@
     side = (board >= half).astype(jnp.int32)
     hub = half - 1 + side
     is_hub = board == hub
-    member = (board - side * half) * plane + seat
-
-    def at(board_index, seat_index):
-        return (lax.div(seat_index, cuts_count), board_index, lax.rem(seat_index, cuts_count))
+    hub_row = (half - 1) * (1 - side)
+    row = board - side * half
+    member = row * plane + seat
+
+    def toggled(value, mask):
+        return value if mask == 0 else lax.bitwise_xor(value, mask)
+
+    def far_first(masks):
+        order = sorted(masks, key=lambda mask: -bin(mask).count("1"))
+        across = [mask for mask in order if mask % cuts_count > 1]
+        rest = [mask for mask in order if mask % cuts_count <= 1]
+        mixed = []
+        while across or rest:
+            mixed += across[:1] + rest[:1]
+            across, rest = across[1:], rest[1:]
+        return mixed
+
+    def seat_of(mask):
+        c, k = toggled(chip, mask // cuts_count), toggled(cuts, mask % cuts_count)
+        return c, k, c * cuts_count + k
+
+    def everyone(boards, act):
+        def on_board(i, carry):
+            where = boards + i
+            for c in range(chip_count):
+                for k in range(cuts_count):
+                    @pl.when((where != board) | (chip != c) | (cuts != k))
+                    def _(c=c, k=k):
+                        act((c, where, k))
+
+            return carry
+
+        return lambda count: lax.fori_loop(0, count, on_board, 0)
 
     def x_copy(i):
         part = pl.ds(i * tile, tile)
@@ -76,12 +108,7 @@
 
     barrier = pltpu.get_barrier_semaphore()
 
-    def greet(offset, carry):
-        peer = lax.rem(me + offset, number)
-        pl.semaphore_signal(barrier, inc=1, device_id=at(lax.div(peer, plane), lax.rem(peer, plane)), device_id_type=MESH)
-        return carry
-
-    lax.fori_loop(1, number, greet, 0)
+    everyone(0, lambda device: pl.semaphore_signal(barrier, inc=1, device_id=device, device_id_type=MESH))(board_count)
     kind = lax.broadcasted_iota(jnp.int32, (CLUSTERS, LANES), 0)
     facts[me] = jnp.where(kind == id_ref[0], count_ref[0].astype(jnp.float32), 0.0)
 
@@ -102,7 +129,6 @@
     w_hi[...] = high
     w_lo[...] = low
     lower_copy.wait()
-    target_copy.wait()
     scale = -LR / count_rows
 
     def error(step, part, h_hi, h_lo):
@@ -116,41 +142,67 @@
     def gradient(part):
         return dot(hid_t_hi[part, :], err_hi[...]) + dot(hid_t_hi[part, :], err_lo[...]) + dot(hid_t_lo[part, :], err_hi[...])
 
-    for i in range(tiles):
-        part = pl.ds(i * tile, tile)
-        x_copy(i).wait()
-        h_hi, h_lo = halves(jnp.tanh(dot(x_buf[part, :], lower[...])))
+    def keep(part, product):
+        h_hi, h_lo = halves(jnp.tanh(product))
         hid_hi[part, :] = h_hi
         hid_lo[part, :] = h_lo
         hid_t_hi[:, part] = h_hi.T
         hid_t_lo[:, part] = h_lo.T
-        error(0, part, h_hi, h_lo)
+        return h_hi, h_lo
+
+    parts = [pl.ds(i * tile, tile) for i in range(tiles)]
+    for i in range(WAIT):
+        x_copy(i).wait()
+    kept = None
+    for i in range(tiles):
+        if i == WAIT:
+            for k in range(WAIT, tiles):
+                x_copy(k).wait()
+            target_copy.wait()
+        product = dot(x_buf[parts[i], :], lower[...])
+        if kept is not None:
+            error(0, parts[i - 1], *kept)
+        kept = keep(parts[i], product)
+    if WAIT >= tiles:
+        target_copy.wait()
+    error(0, parts[-1], *kept)
 
     pl.semaphore_wait(barrier, number - 1)
 
-    def tell(offset, carry):
-        peer = lax.rem(seat + offset, plane)
-        for where in (half - 1, half):
-            @pl.when((offset > 0) | (board != where))
-            def _():
-                pltpu.make_async_remote_copy(
-                    src_ref=facts.at[me], dst_ref=facts.at[me], send_sem=fact_send, recv_sem=fact_recv,
-                    device_id=at(where, peer), device_id_type=MESH,
-                ).start()
-        return carry
-
-    lax.fori_loop(0, plane, tell, 0)
+    def tell(device):
+        pltpu.make_async_remote_copy(
+            src_ref=facts.at[me], dst_ref=facts.at[me], send_sem=fact_send, recv_sem=fact_recv,
+            device_id=device, device_id_type=MESH,
+        ).start()
+
+    everyone(half - 1, tell)(2)
 
     def rows_of(k, seat_index):
-        return pl.ds(pl.multiple_of(k * block + seat_index * share, 8), share)
-
-    def give_share(k, offset):
-        peer = lax.rem(seat + offset, plane)
+        return pl.ds(pl.multiple_of(lax.div(k, groups) * block + seat_index * share, 8), share)
+
+    def columns_of(k):
+        return pl.ds(pl.multiple_of(lax.rem(k, groups) * columns, LANES), columns)
+
+    def give_share(k, mask):
+        c, z, peer = seat_of(mask)
         pltpu.make_async_remote_copy(
-            src_ref=delta.at[rows_of(k, peer)], dst_ref=inbox.at[k, member],
+            src_ref=delta.at[rows_of(k, peer), columns_of(k)], dst_ref=inbox.at[k, member],
             send_sem=share_send, recv_sem=share_recv.at[k],
-            device_id=at(hub, peer), device_id_type=MESH,
+            device_id=(c, hub, z), device_id_type=MESH,
         ).start()
+
+    def give_shares(k):
+        @pl.when(is_hub)
+        def _():
+            inbox[k, member] = delta[rows_of(k, seat), columns_of(k)]
+
+        for mask in far_first(range(plane)):
+            if mask > 0:
+                give_share(k, mask)
+            else:
+                @pl.when(jnp.logical_not(is_hub))
+                def _():
+                    give_share(k, 0)
 
     grad_rows = min(GRAD_ROWS, hid)
     for step in range(steps):
@@ -169,28 +221,25 @@
                 w_hi[part, :] = high
                 w_lo[part, :] = low
             else:
-                for k in range(i * grad_rows // block, (i + 1) * grad_rows // block):
-                    @pl.when(is_hub)
-                    def _(k=k):
-                        inbox[k, member] = delta[rows_of(k, seat), :]
-
-                    @pl.when(jnp.logical_not(is_hub))
-                    def _(k=k):
-                        give_share(k, 0)
-
-                    for offset in range(1, plane):
-                        give_share(k, offset)
+                def send(k, carry):
+                    give_shares(k)
+                    return carry
+
+                per_row = groups * grad_rows // block
+                lax.fori_loop(i * per_row, (i + 1) * per_row, send, 0)
 
     def arrived(ref, sem):
         pltpu.make_async_copy(ref, ref, sem).wait()
 
-    def wide(row):
-        return jnp.concatenate([row] * (width // LANES), axis=1)
+    moved = pl.ds(0, hid // plane * (plane - 1))
+
+    def wide(line):
+        return line if columns == LANES else jnp.concatenate([line] * (columns // LANES), axis=1)
 
     def pair_copy(k):
         return pltpu.make_async_remote_copy(
             src_ref=own.at[k], dst_ref=other.at[k], send_sem=pair_send.at[k], recv_sem=pair_recv.at[k],
-            device_id=at(board_count - 1 - hub, seat), device_id_type=MESH,
+            device_id=(chip, board_count - 1 - hub, cuts), device_id_type=MESH,
         )
 
     @pl.when(is_hub)
@@ -204,7 +253,7 @@
 
         def add_up(k):
             arrived(inbox.at[k, pl.ds(0, members - 1)], share_recv.at[k])
-            sums = [jnp.zeros((share, width), jnp.float32)] * CLUSTERS
+            sums = [jnp.zeros((share, columns), jnp.float32)] * CLUSTERS
             for t in range(members):
                 value = inbox[k, t]
                 for c in range(CLUSTERS):
@@ -221,32 +270,35 @@
                 for c in range(1, CLUSTERS):
                     value = value + wide(chosen[t, c : c + 1, :]) * total[c]
                 outbox[k, t] = value
-            result[rows_of(k, seat), :] = outbox[k, member]
-
-            def give(offset, carry):
-                target_member = lax.rem(member + offset, members)
+            result[rows_of(k, seat), columns_of(k)] = outbox[k, member]
+            for mask in far_first(range(1, members)):
+                c, z, peer = seat_of(mask % plane)
+                peer_row = toggled(hub_row, mask // plane)
                 pltpu.make_async_remote_copy(
-                    src_ref=outbox.at[k, target_member], dst_ref=result.at[rows_of(k, seat)],
+                    src_ref=outbox.at[k, peer_row * plane + peer], dst_ref=result.at[rows_of(k, seat), columns_of(k)],
                     send_sem=back_send, recv_sem=back_recv,
-                    device_id=at(side * half + lax.div(target_member, plane), lax.rem(target_member, plane)), device_id_type=MESH,
+                    device_id=(c, side * half + peer_row, z), device_id_type=MESH,
                 ).start()
-                return carry
-
-            lax.fori_loop(1, members, give, 0)
-
-        def tick(step, carry):
-            @pl.when(step < chunks)
-            def _():
-                add_up(step)
-
-            @pl.when(step >= LAG)
-            def _():
-                give_back(step - LAG)
-
+
+        lag = min(LAG, chunks)
+
+        def first_ticks(k, carry):
+            add_up(k)
             return carry
 
-        lax.fori_loop(0, chunks + LAG, tick, 0)
-        arrived(result.at[pl.ds(0, chunks * (plane - 1) * share)], back_recv)
+        def ticks(k, carry):
+            add_up(k)
+            give_back(k - lag)
+            return carry
+
+        def last_ticks(k, carry):
+            give_back(k)
+            return carry
+
+        lax.fori_loop(0, lag, first_ticks, 0)
+        lax.fori_loop(lag, chunks, ticks, 0)
+        lax.fori_loop(chunks - lag, chunks, last_ticks, 0)
+        arrived(result.at[moved], back_recv)
 
     @pl.when(jnp.logical_not(is_hub))
     def _():
@@ -256,7 +308,7 @@
 
     @pl.when(is_hub)
     def _():
-        arrived(delta.at[pl.ds(0, chunks * (plane - 1) * share)], share_send)
+        arrived(delta.at[moved], share_send)
         arrived(facts.at[pl.ds(0, 2 * plane - 1)], fact_send)
         for k in range(chunks):
             arrived(own.at[k], pair_send.at[k])
@@ -276,7 +328,8 @@
     number = plane * sizes[1]
     members = number // 2
     share = SHARE
-    chunks = hid // (plane * share)
+    columns = COLUMNS
+    chunks = hid // (plane * share) * (width // columns)
     tiles = pool // min(TILE, pool)
     vmem = pl.BlockSpec(memory_space=pltpu.VMEM)
     smem = pl.BlockSpec(memory_space=pltpu.SMEM)
@@ -307,16 +360,16 @@
             pltpu.VMEM((hid, width), full_type),
             pltpu.VMEM((number, CLUSTERS, LANES), full_type),
             pltpu.VMEM((members, CLUSTERS, LANES), full_type),
-            pltpu.VMEM((chunks, members, share, width), full_type),
-            pltpu.VMEM((chunks, CLUSTERS, share, width), full_type),
-            pltpu.VMEM((chunks, CLUSTERS, share, width), full_type),
-            pltpu.VMEM((chunks, members, share, width), full_type),
+            pltpu.VMEM((chunks, members, share, columns), full_type),
+            pltpu.VMEM((chunks, CLUSTERS, share, columns), full_type),
+            pltpu.VMEM((chunks, CLUSTERS, share, columns), full_type),
+            pltpu.VMEM((chunks, members, share, columns), full_type),
             pltpu.VMEM((hid, width), full_type),
             pltpu.SemaphoreType.DMA((tiles,)),
             pltpu.SemaphoreType.DMA((4,)),
             one, one, one, many, many, many, one, one,
         ],
-        compiler_params=pltpu.CompilerParams(collective_id=0, has_side_effects=True, vmem_limit_bytes=56 * 2**20),
+        compiler_params=pltpu.CompilerParams(collective_id=0, has_side_effects=True, vmem_limit_bytes=LIMIT * 2**20),
     )(features, lower_weight, targets, head_weight, batch_rows, sample_counts, cluster_ids)
 
 

time: 45 us -> 40.5 us (0.900)
  Pallas kernels: 41.6 us -> 37.5 us
    pallas_call x1, Pallas kernels: 41.6 us -> 37.5 us  [federated_round(): pl.pallas_call(functools.partial(round_kernel, sizes), name='federated_ro...]
    unnamed x1 -> x3, local copies, waits for them, and re-layouts: 1.87 us -> 1.49 us
where the time goes in v2:
time: 40.5 us; the launch traced here: 40.3 us
  Pallas kernels  37.5 us (93%)
  local copies, waits for them, and re-layouts  1.49 us (4%)
  between operations  1.31 us (3%)
    pallas_call x1, Pallas kernels, federated_round(): pl.pallas_call(functools.partial(round_kernel, sizes), name='federated_ro...  37.5 us
    unnamed x3, local copies, waits for them, and re-layouts  1.49 us

profile of v2, /device:TPU:0, one launch (start us, length us, event | category | flops | bytes accessed | tf_op | source)
XLA Modules:
  0.0 40.3 jit_solution(1101052898838716018)
XLA Ops:
  1.3 0.0 copy-start
  1.3 0.7 %copy-done = s32[1,2,1024]{2,1,0:T(2,128)S(1)} copy-done((s32[1,2,1024]{2,1,0:T(2,128)S(1)}, s32[1,2,1024]{2,1,0:T(2,128)}, u32[]{:S(2)}) %copy-start) | copy-done | bytes 8216
  2.0 37.5 %federated_round.1 = f32[1,512,256]{2,1,0:T(8,128)S(1)} custom-call(bf16[1,2048,1024]{2,1,0:T(8,128)(2,1)} %x_hbm.1, bf16[1,1024,512]{2,1,0:T(8,128)(2,1)} %lower_hbm.1, bf16[1,2048,256]{2,1,0:T(8,128)(2,1)} %target_hbm.1, f32[1,512,256]{2,1,0:T(8,128)} %head_hbm.1, s32[1,2,1024]{2,1,0:T(2,128)S(1)} %copy-done, s32[1]{0:T(128)S(6)} %copy.9.count_ref, ...), custom_call_target="tpu_custom_call" | custom-call | tf_op jit(solution)/shard_map/federated_round/pallas_call | solution.py:339
  39.5 0.8 %copy.11 = f32[1,512,256]{2,1,0:T(8,128)} copy(f32[1,512,256]{2,1,0:T(8,128)S(1)} %federated_round.1) | data formatting | bytes 1048576
Async XLA Ops:
  1.3 0.7 %copy-start = (s32[1,2,1024]{2,1,0:T(2,128)S(1)}, s32[1,2,1024]{2,1,0:T(2,128)}, u32[]{:S(2)}) copy-start(s32[1,2,1024]{2,1,0:T(2,128)} %rows_hbm.1) | copy-start | bytes 24580

commit v3 on v2

--- a/solution.py
+++ b/solution.py
@@ -14,9 +14,9 @@
 GRAD_ROWS = 256
 SHARE = 8
 COLUMNS = 128
-LAG = 4
+LAG = 6
 LIMIT = 53
-WAIT = 1
+WAIT = 2
 MESH = pl.DeviceIdType.MESH
 
 
@@ -32,7 +32,7 @@
 
 def round_kernel(
     sizes, x_hbm, lower_hbm, target_hbm, head_hbm, rows_hbm, count_ref, id_ref, out_ref,
-    x_buf, lower, target, head, rows_ref, hid_hi, hid_lo, hid_t_hi, hid_t_lo, drawn, w_hi, w_lo, err_hi, err_lo, delta,
+    x_buf, lower, target, head, rows_ref, hid_hi, hid_lo, hid_t_hi, hid_t_lo, drawn, w_first, w_pack, low_rest, err_pack, delta,
     facts, chosen, inbox, own, other, outbox, result,
     x_sem, in_sem, fact_send, fact_recv, share_send, share_recv, pair_send, pair_recv, back_send, back_recv,
 ):
@@ -125,22 +125,39 @@
             drawn[step, j * LANES : (j + 1) * LANES, :] = jnp.broadcast_to(table[:, j : j + 1], (LANES, LANES))
 
     head_copy.wait()
-    high, low = halves(head[...])
-    w_hi[...] = high
-    w_lo[...] = low
+    def wide(line):
+        return line if columns == LANES else jnp.concatenate([line] * (columns // LANES), axis=1)
+
+    def lanes(j):
+        return pl.ds(j * columns, columns)
+
+    here, rest = pl.ds(0, columns), pl.ds(columns, columns)
+    for j in range(groups):
+        high, low = halves(head[:, lanes(j)])
+        w_first[:, lanes(j)] = high
+        w_pack[j, :, here] = high
+        w_pack[j, :, rest] = low
     lower_copy.wait()
     scale = -LR / count_rows
 
-    def error(step, part, h_hi, h_lo):
-        err = dot(h_hi, w_hi[...]) + dot(h_hi, w_lo[...]) + dot(h_lo, w_hi[...])
-        err = err - target[part, :].astype(jnp.float32)
-        err = err * jnp.concatenate([drawn[step, part, :]] * (width // LANES), axis=1) * scale
+    def error(step, j, part, h_hi, low_term):
+        both = dot(h_hi, w_pack[j])
+        err = both[:, :columns] + both[:, columns:] + low_term
+        err = err - target[part, lanes(j)].astype(jnp.float32)
+        err = err * wide(drawn[step, part, :]) * scale
         e_hi, e_lo = halves(err)
-        err_hi[part, :] = e_hi
-        err_lo[part, :] = e_lo
+        err_pack[part, here] = e_hi
+        err_pack[part, rest] = e_lo
+
+    def first_error(part, h_hi, h_lo):
+        low = dot(h_lo, w_first[...])
+        for j in range(1, groups):
+            low_rest[j - 1, part, :] = low[:, j * columns : (j + 1) * columns]
+        error(0, 0, part, h_hi, low[:, :columns])
 
     def gradient(part):
-        return dot(hid_t_hi[part, :], err_hi[...]) + dot(hid_t_hi[part, :], err_lo[...]) + dot(hid_t_lo[part, :], err_hi[...])
+        both = dot(hid_t_hi[part, :], err_pack[...])
+        return both[:, :columns] + both[:, columns:] + dot(hid_t_lo[part, :], err_pack[:, here])
 
     def keep(part, product):
         h_hi, h_lo = halves(jnp.tanh(product))
@@ -151,21 +168,22 @@
         return h_hi, h_lo
 
     parts = [pl.ds(i * tile, tile) for i in range(tiles)]
-    for i in range(WAIT):
+    for i in range(min(WAIT, tiles)):
         x_copy(i).wait()
     kept = None
     for i in range(tiles):
         if i == WAIT:
             for k in range(WAIT, tiles):
                 x_copy(k).wait()
+        if i == 1:
             target_copy.wait()
         product = dot(x_buf[parts[i], :], lower[...])
         if kept is not None:
-            error(0, parts[i - 1], *kept)
+            first_error(parts[i - 1], *kept)
         kept = keep(parts[i], product)
-    if WAIT >= tiles:
+    if tiles == 1:
         target_copy.wait()
-    error(0, parts[-1], *kept)
+    first_error(parts[-1], *kept)
 
     pl.semaphore_wait(barrier, number - 1)
 
@@ -178,15 +196,18 @@
     everyone(half - 1, tell)(2)
 
     def rows_of(k, seat_index):
-        return pl.ds(pl.multiple_of(lax.div(k, groups) * block + seat_index * share, 8), share)
+        return pl.ds(pl.multiple_of(lax.rem(k, chunks // groups) * block + seat_index * share, 8), share)
+
+    def group_of(k):
+        return lax.div(k, chunks // groups)
 
     def columns_of(k):
-        return pl.ds(pl.multiple_of(lax.rem(k, groups) * columns, LANES), columns)
+        return pl.ds(pl.multiple_of(group_of(k) * columns, LANES), columns)
 
     def give_share(k, mask):
         c, z, peer = seat_of(mask)
         pltpu.make_async_remote_copy(
-            src_ref=delta.at[rows_of(k, peer), columns_of(k)], dst_ref=inbox.at[k, member],
+            src_ref=delta.at[group_of(k), rows_of(k, peer)], dst_ref=inbox.at[k, member],
             send_sem=share_send, recv_sem=share_recv.at[k],
             device_id=(c, hub, z), device_id_type=MESH,
         ).start()
@@ -194,7 +215,7 @@
     def give_shares(k):
         @pl.when(is_hub)
         def _():
-            inbox[k, member] = delta[rows_of(k, seat), columns_of(k)]
+            inbox[k, member] = delta[group_of(k), rows_of(k, seat), :]
 
         for mask in far_first(range(plane)):
             if mask > 0:
@@ -205,36 +226,36 @@
                     give_share(k, 0)
 
     grad_rows = min(GRAD_ROWS, hid)
-    for step in range(steps):
-        if step > 0:
-            for i in range(tiles):
-                part = pl.ds(i * tile, tile)
-                error(step, part, hid_hi[part, :], hid_lo[part, :])
-        for i in range(hid // grad_rows):
-            part = pl.ds(i * grad_rows, grad_rows)
-            value = gradient(part)
-            if step > 0:
-                value = value + delta[part, :]
-            delta[part, :] = value
-            if step + 1 < steps:
-                high, low = halves(head[part, :] + value)
-                w_hi[part, :] = high
-                w_lo[part, :] = low
-            else:
-                def send(k, carry):
-                    give_shares(k)
-                    return carry
-
-                per_row = groups * grad_rows // block
-                lax.fori_loop(i * per_row, (i + 1) * per_row, send, 0)
+    row_blocks = chunks // groups
+    for j in range(groups):
+        for step in range(steps):
+            for part in parts:
+                if step > 0:
+                    error(step, j, part, hid_hi[part, :], dot(hid_lo[part, :], w_pack[j, :, here]))
+                elif j > 0:
+                    error(step, j, part, hid_hi[part, :], low_rest[j - 1, part, :])
+            for i in range(hid // grad_rows):
+                part = pl.ds(i * grad_rows, grad_rows)
+                value = gradient(part)
+                if step > 0:
+                    value = value + delta[j, part, :]
+                delta[j, part, :] = value
+                if step + 1 < steps:
+                    high, low = halves(head[part, lanes(j)] + value)
+                    w_pack[j, part, here] = high
+                    w_pack[j, part, rest] = low
+                else:
+                    def send(k, carry):
+                        give_shares(k)
+                        return carry
+
+                    start = j * row_blocks + i * grad_rows // block
+                    lax.fori_loop(start, start + grad_rows // block, send, 0)
 
     def arrived(ref, sem):
         pltpu.make_async_copy(ref, ref, sem).wait()
 
     moved = pl.ds(0, hid // plane * (plane - 1))
-
-    def wide(line):
-        return line if columns == LANES else jnp.concatenate([line] * (columns // LANES), axis=1)
 
     def pair_copy(k):
         return pltpu.make_async_remote_copy(
@@ -308,7 +329,7 @@
 
     @pl.when(is_hub)
     def _():
-        arrived(delta.at[moved], share_send)
+        arrived(delta.at[:, moved], share_send)
         arrived(facts.at[pl.ds(0, 2 * plane - 1)], fact_send)
         for k in range(chunks):
             arrived(own.at[k], pair_send.at[k])
@@ -328,7 +349,8 @@
     number = plane * sizes[1]
     members = number // 2
     share = SHARE
-    columns = COLUMNS
+    columns = min(COLUMNS, width)
+    groups = width // columns
     chunks = hid // (plane * share) * (width // columns)
     tiles = pool // min(TILE, pool)
     vmem = pl.BlockSpec(memory_space=pltpu.VMEM)
@@ -354,10 +376,10 @@
             pltpu.VMEM((hid, pool), half_type),
             pltpu.VMEM((steps, pool, LANES), full_type),
             pltpu.VMEM((hid, width), half_type),
-            pltpu.VMEM((hid, width), half_type),
-            pltpu.VMEM((pool, width), half_type),
-            pltpu.VMEM((pool, width), half_type),
-            pltpu.VMEM((hid, width), full_type),
+            pltpu.VMEM((groups, hid, 2 * columns), half_type),
+            pltpu.VMEM((max(1, groups - 1), pool, columns), full_type),
+            pltpu.VMEM((pool, 2 * columns), half_type),
+            pltpu.VMEM((groups, hid, columns), full_type),
             pltpu.VMEM((number, CLUSTERS, LANES), full_type),
             pltpu.VMEM((members, CLUSTERS, LANES), full_type),
             pltpu.VMEM((chunks, members, share, columns), full_type),

time: 40.5 us -> 39.9 us (0.985)
  Pallas kernels: 37.5 us -> 36.8 us
    pallas_call x1, Pallas kernels: 37.5 us -> 36.8 us  [federated_round(): pl.pallas_call(functools.partial(round_kernel, sizes), name='federated_ro...]
where the time goes in v3:
time: 39.9 us; the launch traced here: 39.6 us
  Pallas kernels  36.8 us (92%)
  local copies, waits for them, and re-layouts  1.49 us (4%)
  between operations  1.31 us (3%)
    pallas_call x1, Pallas kernels, federated_round(): pl.pallas_call(functools.partial(round_kernel, sizes), name='federated_ro...  36.8 us
    unnamed x3, local copies, waits for them, and re-layouts  1.49 us

profile of v3, /device:TPU:0, one launch (start us, length us, event | category | flops | bytes accessed | tf_op | source)
XLA Modules:
  0.0 39.6 jit_solution(4191446791447507947)
XLA Ops:
  1.3 0.0 copy-start
  1.3 0.7 %copy-done = s32[1,2,1024]{2,1,0:T(2,128)S(1)} copy-done((s32[1,2,1024]{2,1,0:T(2,128)S(1)}, s32[1,2,1024]{2,1,0:T(2,128)}, u32[]{:S(2)}) %copy-start) | copy-done | bytes 8216
  2.0 36.8 %federated_round.1 = f32[1,512,256]{2,1,0:T(8,128)S(1)} custom-call(bf16[1,2048,1024]{2,1,0:T(8,128)(2,1)} %x_hbm.1, bf16[1,1024,512]{2,1,0:T(8,128)(2,1)} %lower_hbm.1, bf16[1,2048,256]{2,1,0:T(8,128)(2,1)} %target_hbm.1, f32[1,512,256]{2,1,0:T(8,128)} %head_hbm.1, s32[1,2,1024]{2,1,0:T(2,128)S(1)} %copy-done, s32[1]{0:T(128)S(6)} %copy.9.count_ref, ...), custom_call_target="tpu_custom_call" | custom-call | tf_op jit(solution)/shard_map/federated_round/pallas_call | solution.py:361
  38.8 0.8 %copy.11 = f32[1,512,256]{2,1,0:T(8,128)} copy(f32[1,512,256]{2,1,0:T(8,128)S(1)} %federated_round.1) | data formatting | bytes 1048576
Async XLA Ops:
  1.3 0.7 %copy-start = (s32[1,2,1024]{2,1,0:T(2,128)S(1)}, s32[1,2,1024]{2,1,0:T(2,128)}, u32[]{:S(2)}) copy-start(s32[1,2,1024]{2,1,0:T(2,128)} %rows_hbm.1) | copy-start | bytes 24580

commit v4 on v3

--- a/solution.py
+++ b/solution.py
@@ -12,9 +12,9 @@
 LANES = 128
 TILE = 512
 GRAD_ROWS = 256
-SHARE = 8
+SHARE = 16
 COLUMNS = 128
-LAG = 6
+LAG = 2
 LIMIT = 53
 WAIT = 2
 MESH = pl.DeviceIdType.MESH
@@ -33,7 +33,7 @@
 def round_kernel(
     sizes, x_hbm, lower_hbm, target_hbm, head_hbm, rows_hbm, count_ref, id_ref, out_ref,
     x_buf, lower, target, head, rows_ref, hid_hi, hid_lo, hid_t_hi, hid_t_lo, drawn, w_first, w_pack, low_rest, err_pack, delta,
-    facts, chosen, inbox, own, other, outbox, result,
+    facts, chosen, inbox, own, other, outbox,
     x_sem, in_sem, fact_send, fact_recv, share_send, share_recv, pair_send, pair_recv, back_send, back_recv,
 ):
     pool = x_buf.shape[0]
@@ -225,7 +225,7 @@
                 def _():
                     give_share(k, 0)
 
-    grad_rows = min(GRAD_ROWS, hid)
+    grad_rows = min(max(GRAD_ROWS, block), hid)
     row_blocks = chunks // groups
     for j in range(groups):
         for step in range(steps):
@@ -291,12 +291,12 @@
                 for c in range(1, CLUSTERS):
                     value = value + wide(chosen[t, c : c + 1, :]) * total[c]
                 outbox[k, t] = value
-            result[rows_of(k, seat), columns_of(k)] = outbox[k, member]
+            out_ref[0, rows_of(k, seat), columns_of(k)] = outbox[k, member]
             for mask in far_first(range(1, members)):
                 c, z, peer = seat_of(mask % plane)
                 peer_row = toggled(hub_row, mask // plane)
                 pltpu.make_async_remote_copy(
-                    src_ref=outbox.at[k, peer_row * plane + peer], dst_ref=result.at[rows_of(k, seat), columns_of(k)],
+                    src_ref=outbox.at[k, peer_row * plane + peer], dst_ref=out_ref.at[0, rows_of(k, seat), columns_of(k)],
                     send_sem=back_send, recv_sem=back_recv,
                     device_id=(c, side * half + peer_row, z), device_id_type=MESH,
                 ).start()
@@ -319,13 +319,11 @@
         lax.fori_loop(0, lag, first_ticks, 0)
         lax.fori_loop(lag, chunks, ticks, 0)
         lax.fori_loop(chunks - lag, chunks, last_ticks, 0)
-        arrived(result.at[moved], back_recv)
+        arrived(out_ref.at[0, moved], back_recv)
 
     @pl.when(jnp.logical_not(is_hub))
     def _():
-        arrived(result, back_recv)
-
-    out_ref[0] = result[...]
+        arrived(out_ref.at[0], back_recv)
 
     @pl.when(is_hub)
     def _():
@@ -348,7 +346,7 @@
     plane = sizes[0] * sizes[2]
     number = plane * sizes[1]
     members = number // 2
-    share = SHARE
+    share = min(SHARE, hid // plane)
     columns = min(COLUMNS, width)
     groups = width // columns
     chunks = hid // (plane * share) * (width // columns)
@@ -386,7 +384,6 @@
             pltpu.VMEM((chunks, CLUSTERS, share, columns), full_type),
             pltpu.VMEM((chunks, CLUSTERS, share, columns), full_type),
             pltpu.VMEM((chunks, members, share, columns), full_type),
-            pltpu.VMEM((hid, width), full_type),
             pltpu.SemaphoreType.DMA((tiles,)),
             pltpu.SemaphoreType.DMA((4,)),
             one, one, one, many, many, many, one, one,

time: 39.9 us -> 39.4 us (0.987)
  Pallas kernels: 36.8 us -> 36.4 us
    pallas_call x1, Pallas kernels: 36.8 us -> 36.4 us  [federated_round(): pl.pallas_call(functools.partial(round_kernel, sizes), name='federated_ro...]
where the time goes in v4:
time: 39.4 us; the launch traced here: 39.2 us
  Pallas kernels  36.4 us (92%)
  local copies, waits for them, and re-layouts  1.49 us (4%)
  between operations  1.31 us (3%)
    pallas_call x1, Pallas kernels, federated_round(): pl.pallas_call(functools.partial(round_kernel, sizes), name='federated_ro...  36.4 us
    unnamed x3, local copies, waits for them, and re-layouts  1.49 us

profile of v4, /device:TPU:0, one launch (start us, length us, event | category | flops | bytes accessed | tf_op | source)
XLA Modules:
  0.0 39.2 jit_solution(1331192894500723571)
XLA Ops:
  1.3 0.0 copy-start
  1.3 0.7 %copy-done = s32[1,2,1024]{2,1,0:T(2,128)S(1)} copy-done((s32[1,2,1024]{2,1,0:T(2,128)S(1)}, s32[1,2,1024]{2,1,0:T(2,128)}, u32[]{:S(2)}) %copy-start) | copy-done | bytes 8216
  2.0 36.4 %federated_round.1 = f32[1,512,256]{2,1,0:T(8,128)S(1)} custom-call(bf16[1,2048,1024]{2,1,0:T(8,128)(2,1)} %x_hbm.1, bf16[1,1024,512]{2,1,0:T(8,128)(2,1)} %lower_hbm.1, bf16[1,2048,256]{2,1,0:T(8,128)(2,1)} %target_hbm.1, f32[1,512,256]{2,1,0:T(8,128)} %head_hbm.1, s32[1,2,1024]{2,1,0:T(2,128)S(1)} %copy-done, s32[1]{0:T(128)S(6)} %copy.9.count_ref, ...), custom_call_target="tpu_custom_call" | custom-call | tf_op jit(solution)/shard_map/federated_round/pallas_call | solution.py:359
  38.4 0.8 %copy.11 = f32[1,512,256]{2,1,0:T(8,128)} copy(f32[1,512,256]{2,1,0:T(8,128)S(1)} %federated_round.1) | data formatting | bytes 1048576
Async XLA Ops:
  1.3 0.7 %copy-start = (s32[1,2,1024]{2,1,0:T(2,128)S(1)}, s32[1,2,1024]{2,1,0:T(2,128)}, u32[]{:S(2)}) copy-start(s32[1,2,1024]{2,1,0:T(2,128)} %rows_hbm.1) | copy-start | bytes 24580
